TPU v7x, 128 devices: a whole 4x4x4 slice. The times are simulated.
128 devices in a mesh: batch: 1, col: 16 (over z, y), row: 8 (over x, core).
Axes of the slice: x: 4, y: 4, z: 4, core: 2. Of those that a mesh axis runs over, the one named last changes fastest.
Arguments:
- d_inv: bfloat16 [64, 1024, 1024], P(('batch', 'row'))
- l_blk: bfloat16 [64, 1024, 1024], P(('batch', 'row'))
- u_blk: bfloat16 [64, 1024, 1024], P(('batch', 'row'))
- rhs_blk: float32 [64, 1024, 1536], P(('batch', 'row'), None, 'col')
- x_init: float32 [64, 1024, 1536], P(('batch', 'row'), None, 'col')
Outputs:
- output: float32 [64, 1024, 1536], P(('batch', 'row'), None, 'col')
All inputs are finite; a program needn't handle non-finite values.
Results may differ from a plain program's by a relative error of at most 0.0123155.
Values are sent between devices in bfloat16 or wider.
A program may use at most 1 GiB of HBM per device.

v0:
```python
import jax
import jax.numpy as jnp
from jax import lax
from jax.sharding import PartitionSpec as P

SWEEPS = 4


def row_step(x_left, row_in):
    d_i, l_i, u_i, f_i, x_right = row_in
    t_i = (f_i
           - jnp.dot(l_i, x_left.astype(jnp.bfloat16), preferred_element_type=jnp.float32)
           - jnp.dot(u_i, x_right.astype(jnp.bfloat16), preferred_element_type=jnp.float32))
    x_i = jnp.dot(d_i, t_i.astype(jnp.bfloat16), preferred_element_type=jnp.float32)
    return x_i, x_i


def solution(mesh):
    chain_len = mesh.shape["row"]
    mat_spec = P(("batch", "row"), None, None)
    vec_spec = P(("batch", "row"), None, "col")
    fwd_perm = [(src_dev, src_dev + 1) for src_dev in range(chain_len - 1)]
    back_perm = [(src_dev + 1, src_dev) for src_dev in range(chain_len - 1)]

    def device_fn(d_inv, l_blk, u_blk, rhs_blk, x_init):
        chain_pos = lax.axis_index("row")
        zero_blk = jnp.zeros(x_init.shape[1:], jnp.float32)
        x_cur = x_init
        for sweep_idx in range(SWEEPS):
            from_right = lax.ppermute(x_cur[0], "row", back_perm)
            x_right = jnp.concatenate([x_cur[1:], from_right[None]], axis=0)

            def local_sweep(x_left, x_right=x_right):
                _, x_new = lax.scan(row_step, x_left, (d_inv, l_blk, u_blk, rhs_blk, x_right))
                return x_new

            def run_stage(stage_idx, stage_state, local_sweep=local_sweep):
                x_run, x_left = stage_state
                x_run = lax.cond(chain_pos == stage_idx, lambda: local_sweep(x_left), lambda: x_run)
                x_left = lax.ppermute(x_run[-1], "row", fwd_perm)
                return x_run, x_left

            x_cur, _ = lax.fori_loop(0, chain_len, run_stage, (x_cur, zero_blk))
        return x_cur

    return jax.shard_map(device_fn, mesh=mesh, in_specs=(mat_spec, mat_spec, mat_spec, vec_spec, vec_spec), out_specs=vec_spec, check_vma=False)
```

profile of v0, /device:TPU:23, one launch (start us, length us, event | category | flops | bytes accessed | tf_op | source)
XLA Modules:
  0.0 1622.1 jit_solution(17920857290418646356)
XLA Ops:
  17.3 525.6 %while.120 = (s32[]{:T(128)}, f32[8,1024,96]{1,2,0:T(8,128)}, bf16[1024,96]{0,1:T(8,128)(2,1)S(1)}, s32[]{:T(128)}, bf16[8,1024,1024]{2,1,0:T(8,128)(2,1)}, /*in...) while((s32[]{:T(128)}, f32[8,1024,96]{1,2,0:T(8,128)}, ...), condition=%wide.region_5.6_spmd, body=%wide.region_0.5_spmd.sunk | while | flops 604372992 | bytes 9964928 | solution.py:43
  24.1 5.4 collective-permute-done.3
  31.8 5.7 collective-permute-done.3
  39.8 5.7 collective-permute-done.3
  47.9 5.7 collective-permute-done.3
  55.9 5.7 collective-permute-done.3
  63.9 413.9 %collective-permute-done.3 = bf16[1024,96]{0,1:T(8,128)(2,1)S(1)} collective-permute-done((bf16[1024,96]{0,1:T(8,128)(2,1)S(1)}, bf16[1024,96]{0,1:T(8,128)(2,1)S(1)}, u32[]{:S(2)}, u32[]{:S(2)}) %collective-permute-start.3) | collective-permute-done | bytes 196640 | tf_op jit(solution)/shard_map/while/body/eval_jaxpr/ppermute | solution.py:40
  477.8 60.7 %conditional.8 = (f32[8,1024,96]{1,2,0:T(8,128)}) conditional(s32[]{:T(128)} %convert_element_type.132, f32[8,1024,96]{1,2,0:T(8,128)} %get-tuple-element.1636, (bf16[8,1024,1024]{2,1,0:T(8,128)(2,1)}, f32[8,1024,96]{2,1,0:T(8,128)}, bf16[8,1024,1024]{2,1,0:T(8,128)(2,1)}, bf16[8,1024,1024]{2,1,0:T(8,128)(2,1)}, bf16[8,1024,96]{2,1,0:T(8,128)(2,1)S(1)}, ...), branch_computations={%region_1.0_spmd, %region_2.4_spmd} | conditional | flops 604372992 | bytes 8785077 | solution.py:39
  477.8 60.7 %while.116 = (s32[]{:T(128)}, bf16[1024,96]{0,1:T(8,128)(2,1)S(1)}, f32[8,1024,96]{1,2,0:T(8,128)}, bf16[8,1024,1024]{2,1,0:T(8,128)(2,1)}, f32[8,1024,96]{2,1,0...) while((s32[]{:T(128)}, bf16[1024,96]{0,1:T(8,128)(2,1)S(1)}, ...), condition=%wide.region_4.3_spmd, body=%wide.region_3.2_spmd.sunk | while | flops 604372992 | bytes 8784989 | solution.py:34
  487.8 5.2 bitcast_dynamic-update-slice_fusion.11
  502.9 5.2 bitcast_dynamic-update-slice_fusion.11
  518.1 5.2 bitcast_dynamic-update-slice_fusion.11
  533.3 5.2 bitcast_dynamic-update-slice_fusion.11
  549.8 352.8 %while.121 = (s32[]{:T(128)}, f32[8,1024,96]{1,2,0:T(8,128)}, bf16[1024,96]{0,1:T(8,128)(2,1)S(1)}, s32[]{:T(128)}, bf16[8,1024,1024]{2,1,0:T(8,128)(2,1)}, /*in...) while((s32[]{:T(128)}, f32[8,1024,96]{1,2,0:T(8,128)}, ...), condition=%wide.region_11.12_spmd, body=%wide.region_6.11_spmd.sunk | while | flops 604372992 | bytes 9964928 | solution.py:43
  558.8 5.9 collective-permute-done.2
  567.0 5.7 collective-permute-done.2
  575.0 5.7 collective-permute-done.2
  583.0 5.7 collective-permute-done.2
  591.0 5.7 collective-permute-done.2
  599.0 238.5 %collective-permute-done.2 = bf16[1024,96]{0,1:T(8,128)(2,1)S(1)} collective-permute-done((bf16[1024,96]{0,1:T(8,128)(2,1)S(1)}, bf16[1024,96]{0,1:T(8,128)(2,1)S(1)}, u32[]{:S(2)}, u32[]{:S(2)}) %collective-permute-start.2) | collective-permute-done | bytes 196640 | tf_op jit(solution)/shard_map/while/body/eval_jaxpr/ppermute | solution.py:40
  837.5 60.7 %conditional.9 = (f32[8,1024,96]{1,2,0:T(8,128)}) conditional(s32[]{:T(128)} %convert_element_type.133, f32[8,1024,96]{1,2,0:T(8,128)} %get-tuple-element.1666, (bf16[8,1024,1024]{2,1,0:T(8,128)(2,1)}, f32[8,1024,96]{2,1,0:T(8,128)}, bf16[8,1024,1024]{2,1,0:T(8,128)(2,1)}, bf16[8,1024,1024]{2,1,0:T(8,128)(2,1)}, bf16[8,1024,96]{2,1,0:T(8,128)(2,1)S(1)}, ...), branch_computations={%region_7.7_spmd, %region_8.10_spmd} | conditional | flops 604372992 | bytes 8785077 | solution.py:39
  837.5 60.7 %while.117 = (s32[]{:T(128)}, bf16[1024,96]{0,1:T(8,128)(2,1)S(1)}, f32[8,1024,96]{1,2,0:T(8,128)}, bf16[8,1024,1024]{2,1,0:T(8,128)(2,1)}, f32[8,1024,96]{2,1,0...) while((s32[]{:T(128)}, bf16[1024,96]{0,1:T(8,128)(2,1)S(1)}, ...), condition=%wide.region_10.9_spmd, body=%wide.region_9.8_spmd.sunk | while | flops 604372992 | bytes 8784989 | solution.py:34
  855.1 5.2 bitcast_dynamic-update-slice_fusion.10
  870.3 5.2 bitcast_dynamic-update-slice_fusion.10
  885.5 5.2 bitcast_dynamic-update-slice_fusion.10
  909.6 352.8 %while.122 = (s32[]{:T(128)}, f32[8,1024,96]{1,2,0:T(8,128)}, bf16[1024,96]{0,1:T(8,128)(2,1)S(1)}, s32[]{:T(128)}, bf16[8,1024,1024]{2,1,0:T(8,128)(2,1)}, /*in...) while((s32[]{:T(128)}, f32[8,1024,96]{1,2,0:T(8,128)}, ...), condition=%wide.region_17.18_spmd, body=%wide.region_12.17_spmd.sunk | while | flops 604372992 | bytes 9964928 | solution.py:43
  918.5 5.9 collective-permute-done.1
  926.7 5.7 collective-permute-done.1
  934.7 5.7 collective-permute-done.1
  942.7 5.7 collective-permute-done.1
  950.8 5.7 collective-permute-done.1
  958.8 238.5 %collective-permute-done.1 = bf16[1024,96]{0,1:T(8,128)(2,1)S(1)} collective-permute-done((bf16[1024,96]{0,1:T(8,128)(2,1)S(1)}, bf16[1024,96]{0,1:T(8,128)(2,1)S(1)}, u32[]{:S(2)}, u32[]{:S(2)}) %collective-permute-start.1) | collective-permute-done | bytes 196640 | tf_op jit(solution)/shard_map/while/body/eval_jaxpr/ppermute | solution.py:40
  1197.3 60.7 %conditional.10 = (f32[8,1024,96]{1,2,0:T(8,128)}) conditional(s32[]{:T(128)} %convert_element_type.134, f32[8,1024,96]{1,2,0:T(8,128)} %get-tuple-element.1696, (bf16[8,1024,1024]{2,1,0:T(8,128)(2,1)}, f32[8,1024,96]{2,1,0:T(8,128)}, bf16[8,1024,1024]{2,1,0:T(8,128)(2,1)}, bf16[8,1024,1024]{2,1,0:T(8,128)(2,1)}, ...), branch_computations={%region_13.13_spmd, %region_14.16_spmd} | conditional | flops 604372992 | bytes 8785077 | solution.py:39
  1197.3 60.7 %while.118 = (s32[]{:T(128)}, bf16[1024,96]{0,1:T(8,128)(2,1)S(1)}, f32[8,1024,96]{1,2,0:T(8,128)}, bf16[8,1024,1024]{2,1,0:T(8,128)(2,1)}, f32[8,1024,96]{2,1,0...) while((s32[]{:T(128)}, bf16[1024,96]{0,1:T(8,128)(2,1)S(1)}, ...), condition=%wide.region_16.15_spmd, body=%wide.region_15.14_spmd.sunk | while | flops 604372992 | bytes 8784989 | solution.py:34
  1245.2 5.2 bitcast_dynamic-update-slice_fusion.9
  1269.3 352.8 %while.123 = (s32[]{:T(128)}, f32[8,1024,96]{1,2,0:T(8,128)}, bf16[1024,96]{0,1:T(8,128)(2,1)S(1)}, s32[]{:T(128)}, bf16[8,1024,1024]{2,1,0:T(8,128)(2,1)}, /*in...) while((s32[]{:T(128)}, f32[8,1024,96]{1,2,0:T(8,128)}, ...), condition=%wide.region_23.24_spmd, body=%wide.region_18.23_spmd.sunk | while | flops 604372992 | bytes 9964928 | solution.py:43
  1278.2 5.9 collective-permute-done
  1286.4 5.7 collective-permute-done
  1294.5 5.7 collective-permute-done
  1302.5 5.7 collective-permute-done
  1310.5 5.7 collective-permute-done
  1318.5 238.5 %collective-permute-done = bf16[1024,96]{0,1:T(8,128)(2,1)S(1)} collective-permute-done((bf16[1024,96]{0,1:T(8,128)(2,1)S(1)}, bf16[1024,96]{0,1:T(8,128)(2,1)S(1)}, u32[]{:S(2)}, u32[]{:S(2)}) %collective-permute-start) | collective-permute-done | bytes 196640 | tf_op jit(solution)/shard_map/while/body/eval_jaxpr/ppermute | solution.py:40
  1557.0 60.7 %conditional.11 = (f32[8,1024,96]{1,2,0:T(8,128)}) conditional(s32[]{:T(128)} %convert_element_type.135, f32[8,1024,96]{1,2,0:T(8,128)} %get-tuple-element.1726, (bf16[8,1024,1024]{2,1,0:T(8,128)(2,1)}, f32[8,1024,96]{2,1,0:T(8,128)}, bf16[8,1024,1024]{2,1,0:T(8,128)(2,1)}, bf16[8,1024,1024]{2,1,0:T(8,128)(2,1)}, ...), branch_computations={%region_19.19_spmd, %region_20.22_spmd} | conditional | flops 604372992 | bytes 8785077 | solution.py:39
  1557.0 60.7 %while.119 = (s32[]{:T(128)}, bf16[1024,96]{0,1:T(8,128)(2,1)S(1)}, f32[8,1024,96]{1,2,0:T(8,128)}, bf16[8,1024,1024]{2,1,0:T(8,128)(2,1)}, f32[8,1024,96]{2,1,0...) while((s32[]{:T(128)}, bf16[1024,96]{0,1:T(8,128)(2,1)S(1)}, ...), condition=%wide.region_22.21_spmd, body=%wide.region_21.20_spmd.sunk | while | flops 604372992 | bytes 8784989 | solution.py:34
  1566.9 5.2 bitcast_dynamic-update-slice_fusion.8
  1582.1 5.2 bitcast_dynamic-update-slice_fusion.8
  1597.3 5.2 bitcast_dynamic-update-slice_fusion.8
  1612.5 5.2 bitcast_dynamic-update-slice_fusion.8
  (189 shorter events, 315.1 us)
Async XLA Ops:
  1.9 8.6 copy-start
  2.9 12.5 collective-permute-start.4
  18.4 3.3 collective-permute-start.3
  22.8 6.7 collective-permute-start.3
  30.5 7.0 collective-permute-start.3
  38.5 7.0 collective-permute-start.3
  46.5 7.0 collective-permute-start.3
  54.6 7.0 collective-permute-start.3
  62.6 415.2 %collective-permute-start.3 = (bf16[1024,96]{0,1:T(8,128)(2,1)S(1)}, bf16[1024,96]{0,1:T(8,128)(2,1)S(1)}, u32[]{:S(2)}, u32[]{:S(2)}) collective-permute-start(bf16[1024,96]{0,1:T(8,128)(2,1)S(1)} %slice_bitcast_fusion.11), channel_id=1, source_target_pairs={{0,1},{1,2},{2,3},{3,4},{4,5},{5,6},{6,7},{8,9},{9,10},{10,11},{11... | collective-permute-start | bytes 589832 | tf_op jit(solution)/shard_map/while/body/eval_jaxpr/ppermute | solution.py:40
  539.5 3.3 collective-permute-start.3
  546.2 3.2 collective-permute-start.5
  550.9 5.6 collective-permute-start.2
  557.5 7.2 collective-permute-start.2
  565.7 7.0 collective-permute-start.2
  573.7 7.0 collective-permute-start.2
  581.7 7.0 collective-permute-start.2
  589.7 7.0 collective-permute-start.2
  597.7 239.8 %collective-permute-start.2 = (bf16[1024,96]{0,1:T(8,128)(2,1)S(1)}, bf16[1024,96]{0,1:T(8,128)(2,1)S(1)}, u32[]{:S(2)}, u32[]{:S(2)}) collective-permute-start(bf16[1024,96]{0,1:T(8,128)(2,1)S(1)} %slice_bitcast_fusion.12), channel_id=1, source_target_pairs={{0,1},{1,2},{2,3},{3,4},{4,5},{5,6},{6,7},{8,9},{9,10},{10,11},{11... | collective-permute-start | bytes 589832 | tf_op jit(solution)/shard_map/while/body/eval_jaxpr/ppermute | solution.py:40
  899.3 3.3 collective-permute-start.2
  905.9 3.2 collective-permute-start.6
  910.6 5.6 collective-permute-start.1
  917.2 7.2 collective-permute-start.1
  925.4 7.0 collective-permute-start.1
  933.4 7.0 collective-permute-start.1
  941.4 7.0 collective-permute-start.1
  949.5 7.0 collective-permute-start.1
  957.5 239.8 %collective-permute-start.1 = (bf16[1024,96]{0,1:T(8,128)(2,1)S(1)}, bf16[1024,96]{0,1:T(8,128)(2,1)S(1)}, u32[]{:S(2)}, u32[]{:S(2)}) collective-permute-start(bf16[1024,96]{0,1:T(8,128)(2,1)S(1)} %slice_bitcast_fusion.13), channel_id=1, source_target_pairs={{0,1},{1,2},{2,3},{3,4},{4,5},{5,6},{6,7},{8,9},{9,10},{10,11},{11... | collective-permute-start | bytes 589832 | tf_op jit(solution)/shard_map/while/body/eval_jaxpr/ppermute | solution.py:40
  1259.0 3.3 collective-permute-start.1
  1265.6 3.2 collective-permute-start.7
  1270.4 5.6 collective-permute-start
  1276.9 7.2 collective-permute-start
  1285.1 7.0 collective-permute-start
  1293.2 7.0 collective-permute-start
  1301.2 7.0 collective-permute-start
  1309.2 7.0 collective-permute-start
  1317.2 239.8 %collective-permute-start = (bf16[1024,96]{0,1:T(8,128)(2,1)S(1)}, bf16[1024,96]{0,1:T(8,128)(2,1)S(1)}, u32[]{:S(2)}, u32[]{:S(2)}) collective-permute-start(bf16[1024,96]{0,1:T(8,128)(2,1)S(1)} %slice_bitcast_fusion.14), channel_id=1, source_target_pairs={{0,1},{1,2},{2,3},{3,4},{4,5},{5,6},{6,7},{8,9},{9,10},{10,11},{11... | collective-permute-start | bytes 589832 | tf_op jit(solution)/shard_map/while/body/eval_jaxpr/ppermute | solution.py:40
  1618.7 3.3 collective-permute-start
where the time goes:
time: 1630 us; the launch traced here: 1620 us
  waiting for transfers between devices  1270 us (78%)
  matrix products  243 us (15%)
  local copies, waits for them, and re-layouts  55.6 us (3%)
  starting transfers between devices  50.3 us (3%)
    ppermute x32, waiting for transfers between devices, run_stage(): x_left = lax.ppermute(x_run[-1], 'row', fwd_perm)  1270 us
    dot_general x32, matrix products, row_step(): jnp.dot(d_i, t_i.astype(jnp.bfloat16), preferred_element_type=jnp.float32)  167 us
    dot_general x32, matrix products, row_step(): jnp.dot(l_i, x_left.astype(jnp.bfloat16), preferred_element_type=jnp.floa...  75.9 us
    ppermute x32, starting transfers between devices, run_stage(): x_left = lax.ppermute(x_run[-1], 'row', fwd_perm)  41.3 us
  transfers between devices with their start and end apart: 36, of which 35 were waited for; matrix products, arithmetic and copies ran while one was open for 1% of the time, Pallas kernels for 0%

commit v1 on v0

v1 whole, which is shorter than its diff:
```python
import functools

import jax
import jax.numpy as jnp
from jax import lax
from jax.experimental import pallas as pl
from jax.experimental.pallas import tpu as pltpu
from jax.sharding import PartitionSpec as P

SWEEPS = 4
TILE = 256
MESH = pl.DeviceIdType.MESH
F32, BF16 = jnp.float32, jnp.bfloat16


def dot_nn(x, mat):
    return jnp.dot(x, mat, preferred_element_type=F32)


def dot_nt(x, mat):
    return lax.dot_general(x, mat, (((1,), (1,)), ((), ())), preferred_element_type=F32)


def kernel(chain_len, rows, d_hbm, l_hbm, u_hbm, f_hbm, x_hbm, out_hbm,
           d_v, l_v, u_v, f_t, g_t, xs, f_raw, x_raw, x_f32, out_st,
           d_sem, l_sem, u_sem, f_sem, x_sem, out_sem,
           fs_sem, fr_sem, bs_sem, br_sem):
    p = lax.axis_index("row")
    size = d_v.shape[1]
    tiles = size // TILE
    has_left, has_right = p > 0, p < chain_len - 1
    from_left, from_right = rows, rows + SWEEPS

    def mat_copies(i):
        return (pltpu.make_async_copy(u_hbm.at[i], u_v.at[i], u_sem.at[i]),
                pltpu.make_async_copy(l_hbm.at[i], l_v.at[i], l_sem.at[i]),
                pltpu.make_async_copy(d_hbm.at[i], d_v.at[i], d_sem.at[i]))

    def f_copy(i, slot):
        return pltpu.make_async_copy(f_hbm.at[i], f_raw.at[slot], f_sem.at[slot])

    def x_copy(i, slot):
        return pltpu.make_async_copy(x_hbm.at[i], x_raw.at[slot], x_sem.at[slot])

    def send_right(k):
        return pltpu.make_async_remote_copy(
            src_ref=xs.at[rows - 1], dst_ref=xs.at[from_left + k], send_sem=fs_sem.at[k], recv_sem=fr_sem.at[k],
            device_id={"row": p + 1}, device_id_type=MESH)

    def send_left(k):
        return pltpu.make_async_remote_copy(
            src_ref=xs.at[0], dst_ref=xs.at[from_right + k], send_sem=bs_sem.at[k], recv_sem=br_sem.at[k],
            device_id={"row": p - 1}, device_id_type=MESH)

    x_copy(0, 0).start()
    x_copy(1, 1).start()
    f_copy(0, 0).start()
    f_copy(1, 1).start()
    for i in range(2):
        for c in mat_copies(i):
            c.start()

    barrier = pltpu.get_barrier_semaphore()

    @pl.when(has_left)
    def _():
        pl.semaphore_signal(barrier, inc=1, device_id={"row": p - 1}, device_id_type=MESH)

    @pl.when(has_right)
    def _():
        pl.semaphore_signal(barrier, inc=1, device_id={"row": p + 1}, device_id_type=MESH)

    pl.semaphore_wait(barrier, has_left.astype(jnp.int32) + has_right.astype(jnp.int32))

    zero = jnp.zeros(xs.shape[1:], BF16)

    @pl.when(jnp.logical_not(has_left))
    def _():
        for k in range(SWEEPS):
            xs[from_left + k] = zero

    @pl.when(jnp.logical_not(has_right))
    def _():
        for k in range(SWEEPS):
            xs[from_right + k] = zero

    def load_x(i, slot):
        x_copy(i, slot).wait()
        xs[i] = x_raw[slot].T.astype(BF16)

    def transpose_in_place(ref, i):
        def at(a, b):
            return ref.at[i, a * TILE:(a + 1) * TILE, b * TILE:(b + 1) * TILE]
        for a in range(tiles):
            at(a, a)[...] = at(a, a)[...].T
            for b in range(a + 1, tiles):
                upper, lower = at(a, b)[...].T, at(b, a)[...].T
                at(a, b)[...] = lower
                at(b, a)[...] = upper

    load_x(0, 0)
    x_copy(2, 0).start()

    @pl.when(has_left)
    def _():
        send_left(0).start()

    def load_row(i, last=False):
        slot = lax.rem(i, 2)
        if not last:
            @pl.when(i + 2 < rows)
            def _():
                for c in mat_copies(i + 2):
                    c.start()
            load_x(i + 1, 1 - slot)

            @pl.when(i + 3 < rows)
            def _():
                x_copy(i + 3, 1 - slot).start()
        f_copy(i, slot).wait()
        f_t[i] = f_raw[slot].T

        @pl.when(i + 2 < rows)
        def _():
            f_copy(i + 2, slot).start()
        u_c, l_c, d_c = mat_copies(i)
        l_c.wait()
        transpose_in_place(l_v, i)
        d_c.wait()
        transpose_in_place(d_v, i)
        u_c.wait()
        if not last:
            g_t[i] = f_t[i] - dot_nt(xs[i + 1], u_v[i])

    @pl.loop(0, rows - 1)
    def _(i):
        load_row(i)
    load_row(rows - 1, last=True)

    def row(i, left, final):
        t = g_t[i] - dot_nn(xs[left], l_v[i])
        x = dot_nn(t.astype(BF16), d_v[i])
        xs[i] = x.astype(BF16)
        if final:
            st = lax.rem(i, 2)

            @pl.when(i >= 2)
            def _():
                pltpu.make_async_copy(out_st.at[st], out_hbm.at[i - 2], out_sem.at[st]).wait()
            out_st[st] = x.T
            pltpu.make_async_copy(out_st.at[st], out_hbm.at[i], out_sem.at[st]).start()

    def sweep(k, final):
        @pl.when(has_left)
        def _():
            send_left(k).wait_send()
            fwd = pltpu.make_async_remote_copy(
                src_ref=xs.at[rows - 1], dst_ref=xs.at[from_left + k], send_sem=fs_sem.at[k], recv_sem=fr_sem.at[k],
                device_id={"row": p - 1}, device_id_type=MESH)
            fwd.wait_recv()

        @pl.when(jnp.logical_and(has_right, k > 0))
        def _():
            send_right(k - 1).wait_send()

        row(0, from_left + k, final)
        if not final:
            @pl.when(has_left)
            def _():
                send_left(k + 1).start()

        @pl.loop(1, rows - 1)
        def _(i):
            row(i, i - 1, final)

        @pl.when(has_right)
        def _():
            bwd = pltpu.make_async_remote_copy(
                src_ref=xs.at[0], dst_ref=xs.at[from_right + k], send_sem=bs_sem.at[k], recv_sem=br_sem.at[k],
                device_id={"row": p + 1}, device_id_type=MESH)
            bwd.wait_recv()
        last = rows - 1
        g_t[last] = f_t[last] - dot_nt(xs[from_right + k], u_v[last])
        row(last, last - 1, final)

        @pl.when(has_right)
        def _():
            send_right(k).start()

        if not final:
            @pl.loop(0, rows - 1)
            def _(i):
                g_t[i] = f_t[i] - dot_nt(xs[i + 1], u_v[i])

    @pl.loop(0, SWEEPS - 1)
    def _(k):
        sweep(k, False)
    sweep(SWEEPS - 1, True)

    @pl.when(has_right)
    def _():
        send_right(SWEEPS - 1).wait_send()
    for i in (rows - 2, rows - 1):
        pltpu.make_async_copy(out_st.at[i % 2], out_hbm.at[i], out_sem.at[i % 2]).wait()


def solution(mesh):
    chain_len = mesh.shape["row"]
    mat_spec = P(("batch", "row"), None, None)
    vec_spec = P(("batch", "row"), None, "col")

    def device_fn(d_inv, l_blk, u_blk, rhs_blk, x_init):
        rows, size, cols = rhs_blk.shape
        any_spec = pl.BlockSpec(memory_space=pl.ANY)
        mat = pltpu.VMEM((rows, size, size), BF16)
        dma = pltpu.SemaphoreType.DMA
        return pl.pallas_call(
            functools.partial(kernel, chain_len, rows),
            out_shape=jax.ShapeDtypeStruct(rhs_blk.shape, F32),
            in_specs=[any_spec] * 5,
            out_specs=any_spec,
            scratch_shapes=[
                mat, mat, mat,
                pltpu.VMEM((rows, cols, size), F32),
                pltpu.VMEM((rows, cols, size), F32),
                pltpu.VMEM((rows + 2 * SWEEPS, cols, size), BF16),
                pltpu.VMEM((2, size, cols), F32),
                pltpu.VMEM((2, size, cols), F32),
                pltpu.VMEM((8, 128), F32),
                pltpu.VMEM((2, size, cols), F32),
                dma((rows,)), dma((rows,)), dma((rows,)), dma((2,)), dma((2,)), dma((2,)),
                dma((SWEEPS,)), dma((SWEEPS,)), dma((SWEEPS,)), dma((SWEEPS,)),
            ],
            compiler_params=pltpu.CompilerParams(
                collective_id=0, has_side_effects=True, vmem_limit_bytes=67043328),
        )(d_inv, l_blk, u_blk, rhs_blk, x_init)

    return jax.shard_map(device_fn, mesh=mesh, in_specs=(mat_spec, mat_spec, mat_spec, vec_spec, vec_spec),
                         out_specs=vec_spec, check_vma=False)
```

time: 1630 us -> 161 us (0.10)
  waiting for transfers between devices: 1270 us -> 0 us
  matrix products: 243 us -> 0 us
  Pallas kernels: 0 us -> 147 us
  starting transfers between devices: 50.3 us -> 0 us
  local copies, waits for them, and re-layouts: 55.6 us -> 13.6 us
    ppermute x36 -> x0, waiting for transfers between devices: 1270 us -> none  [the longest x32 1270 us: run_stage(): x_left = lax.ppermute(x_run[-1], 'row', fwd_perm)]
    dot_general x64 -> x0, matrix products: 243 us -> none  [the longest x32 167 us: row_step(): jnp.dot(d_i, t_i.astype(jnp.bfloat16), preferred_element_type=jnp.float32)]
    pallas_call x0 -> x1, Pallas kernels: none -> 147 us  [device_fn(): pl.pallas_call(functools.partial(kernel, chain_len, rows), out_shape=jax....]
    ppermute x36 -> x0, starting transfers between devices: 50.3 us -> none  [the longest x32 41.3 us: run_stage(): x_left = lax.ppermute(x_run[-1], 'row', fwd_perm)]
    squeeze x35 -> x0, local copies, waits for them, and re-layouts: 32.6 us -> none  [the longest x32 32.6 us: run_stage(): x_left = lax.ppermute(x_run[-1], 'row', fwd_perm)]
  transfers between devices with their start and end apart: 36 -> 0, of which waited for: 35 -> 0; matrix products, arithmetic and copies ran while one was open for 1% -> 0% of each run, Pallas kernels for 0% -> 0%
where the time goes in v1:
time: 161 us
  Pallas kernels  147 us (91%)
  local copies, waits for them, and re-layouts  13.6 us (8%)
    pallas_call x1, Pallas kernels, device_fn(): pl.pallas_call(functools.partial(kernel, chain_len, rows), out_shape=jax....  147 us
    unnamed x4, local copies, waits for them, and re-layouts  8.39 us
    pallas_call x1, local copies, waits for them, and re-layouts, device_fn(): pl.pallas_call(functools.partial(kernel, chain_len, rows), out_shape=jax....  5.24 us

profile of v1, /device:TPU:23, one launch (start us, length us, event | category | flops | bytes accessed | tf_op | source)
XLA Modules:
  0.0 160.5 jit_solution(10935424859146058430)
XLA Ops:
  0.0 0.0 copy-start
  0.0 5.1 %copy.6.f_hbm = f32[8,1024,96]{2,1,0:T(8,128)} copy(f32[8,1024,96]{1,2,0:T(8,128)} %param.8) | data formatting | bytes 6291456 | tf_op args[3]
  5.1 0.0 copy-done
  5.1 3.3 %copy.7.x_hbm = f32[8,1024,96]{2,1,0:T(8,128)} copy(f32[8,1024,96]{1,2,0:T(8,128)S(1)} %copy-done) | data formatting | bytes 6291456 | tf_op args[4]
  8.4 146.9 %shard_map.55 = f32[8,1024,96]{2,1,0:T(8,128)} custom-call(bf16[8,1024,1024]{2,1,0:T(8,128)(2,1)} %d_hbm.1, bf16[8,1024,1024]{2,1,0:T(8,128)(2,1)} %l_hbm.1, bf16[8,1024,1024]{2,1,0:T(8,128)(2,1)} %u_hbm.1, f32[8,1024,96]{2,1,0:T(8,128)} %copy.6.f_hbm, f32[8,1024,96]{2,1,0:T(8,128)} %copy.7.x_hbm), custom_call_target="tpu_custom_call" | custom-call | tf_op jit(solution)/shard_map/pallas_call | solution.py:217
  155.3 5.2 %copy.8 = f32[8,1024,96]{1,2,0:T(8,128)} copy(f32[8,1024,96]{2,1,0:T(8,128)} %shard_map.55) | data formatting | bytes 6291456 | tf_op jit(solution)/shard_map/pallas_call | solution.py:217
Async XLA Ops:
  0.0 5.1 %copy-start = (f32[8,1024,96]{1,2,0:T(8,128)S(1)}, f32[8,1024,96]{1,2,0:T(8,128)}, u32[]{:S(2)}) copy-start(f32[8,1024,96]{1,2,0:T(8,128)} %param.9) | copy-start | bytes 9437188

commit v2 on v1

--- a/solution.py
+++ b/solution.py
@@ -22,7 +22,7 @@
 
 
 def kernel(chain_len, rows, d_hbm, l_hbm, u_hbm, f_hbm, x_hbm, out_hbm,
-           d_v, l_v, u_v, f_t, g_t, xs, f_raw, x_raw, x_f32, out_st,
+           d_v, l_v, u_v, f_v, g_v, xs, x_raw, out_st,
            d_sem, l_sem, u_sem, f_sem, x_sem, out_sem,
            fs_sem, fr_sem, bs_sem, br_sem):
     p = lax.axis_index("row")
@@ -36,8 +36,8 @@
                 pltpu.make_async_copy(l_hbm.at[i], l_v.at[i], l_sem.at[i]),
                 pltpu.make_async_copy(d_hbm.at[i], d_v.at[i], d_sem.at[i]))
 
-    def f_copy(i, slot):
-        return pltpu.make_async_copy(f_hbm.at[i], f_raw.at[slot], f_sem.at[slot])
+    def f_copy(i):
+        return pltpu.make_async_copy(f_hbm.at[i], f_v.at[i], f_sem.at[i])
 
     def x_copy(i, slot):
         return pltpu.make_async_copy(x_hbm.at[i], x_raw.at[slot], x_sem.at[slot])
@@ -54,8 +54,8 @@
 
     x_copy(0, 0).start()
     x_copy(1, 1).start()
-    f_copy(0, 0).start()
-    f_copy(1, 1).start()
+    f_copy(0).start()
+    f_copy(1).start()
     for i in range(2):
         for c in mat_copies(i):
             c.start()
@@ -86,7 +86,7 @@
 
     def load_x(i, slot):
         x_copy(i, slot).wait()
-        xs[i] = x_raw[slot].T.astype(BF16)
+        xs[i] = x_raw[slot].astype(BF16)
 
     def transpose_in_place(ref, i):
         def at(a, b):
@@ -110,6 +110,7 @@
         if not last:
             @pl.when(i + 2 < rows)
             def _():
+                f_copy(i + 2).start()
                 for c in mat_copies(i + 2):
                     c.start()
             load_x(i + 1, 1 - slot)
@@ -117,12 +118,7 @@
             @pl.when(i + 3 < rows)
             def _():
                 x_copy(i + 3, 1 - slot).start()
-        f_copy(i, slot).wait()
-        f_t[i] = f_raw[slot].T
-
-        @pl.when(i + 2 < rows)
-        def _():
-            f_copy(i + 2, slot).start()
+        f_copy(i).wait()
         u_c, l_c, d_c = mat_copies(i)
         l_c.wait()
         transpose_in_place(l_v, i)
@@ -130,7 +126,7 @@
         transpose_in_place(d_v, i)
         u_c.wait()
         if not last:
-            g_t[i] = f_t[i] - dot_nt(xs[i + 1], u_v[i])
+            g_v[i] = f_v[i] - dot_nt(xs[i + 1], u_v[i])
 
     @pl.loop(0, rows - 1)
     def _(i):
@@ -138,7 +134,7 @@
     load_row(rows - 1, last=True)
 
     def row(i, left, final):
-        t = g_t[i] - dot_nn(xs[left], l_v[i])
+        t = g_v[i] - dot_nn(xs[left], l_v[i])
         x = dot_nn(t.astype(BF16), d_v[i])
         xs[i] = x.astype(BF16)
         if final:
@@ -147,7 +143,7 @@
             @pl.when(i >= 2)
             def _():
                 pltpu.make_async_copy(out_st.at[st], out_hbm.at[i - 2], out_sem.at[st]).wait()
-            out_st[st] = x.T
+            out_st[st] = x
             pltpu.make_async_copy(out_st.at[st], out_hbm.at[i], out_sem.at[st]).start()
 
     def sweep(k, final):
@@ -180,7 +176,7 @@
                 device_id={"row": p + 1}, device_id_type=MESH)
             bwd.wait_recv()
         last = rows - 1
-        g_t[last] = f_t[last] - dot_nt(xs[from_right + k], u_v[last])
+        g_v[last] = f_v[last] - dot_nt(xs[from_right + k], u_v[last])
         row(last, last - 1, final)
 
         @pl.when(has_right)
@@ -190,7 +186,7 @@
         if not final:
             @pl.loop(0, rows - 1)
             def _(i):
-                g_t[i] = f_t[i] - dot_nt(xs[i + 1], u_v[i])
+                g_v[i] = f_v[i] - dot_nt(xs[i + 1], u_v[i])
 
     @pl.loop(0, SWEEPS - 1)
     def _(k):
@@ -210,11 +206,12 @@
     vec_spec = P(("batch", "row"), None, "col")
 
     def device_fn(d_inv, l_blk, u_blk, rhs_blk, x_init):
-        rows, size, cols = rhs_blk.shape
+        rhs_blk, x_init = jnp.swapaxes(rhs_blk, 1, 2), jnp.swapaxes(x_init, 1, 2)
+        rows, cols, size = rhs_blk.shape
         any_spec = pl.BlockSpec(memory_space=pl.ANY)
         mat = pltpu.VMEM((rows, size, size), BF16)
         dma = pltpu.SemaphoreType.DMA
-        return pl.pallas_call(
+        x_final = pl.pallas_call(
             functools.partial(kernel, chain_len, rows),
             out_shape=jax.ShapeDtypeStruct(rhs_blk.shape, F32),
             in_specs=[any_spec] * 5,
@@ -224,16 +221,15 @@
                 pltpu.VMEM((rows, cols, size), F32),
                 pltpu.VMEM((rows, cols, size), F32),
                 pltpu.VMEM((rows + 2 * SWEEPS, cols, size), BF16),
-                pltpu.VMEM((2, size, cols), F32),
-                pltpu.VMEM((2, size, cols), F32),
-                pltpu.VMEM((8, 128), F32),
-                pltpu.VMEM((2, size, cols), F32),
-                dma((rows,)), dma((rows,)), dma((rows,)), dma((2,)), dma((2,)), dma((2,)),
+                pltpu.VMEM((2, cols, size), F32),
+                pltpu.VMEM((2, cols, size), F32),
+                dma((rows,)), dma((rows,)), dma((rows,)), dma((rows,)), dma((2,)), dma((2,)),
                 dma((SWEEPS,)), dma((SWEEPS,)), dma((SWEEPS,)), dma((SWEEPS,)),
             ],
             compiler_params=pltpu.CompilerParams(
                 collective_id=0, has_side_effects=True, vmem_limit_bytes=67043328),
         )(d_inv, l_blk, u_blk, rhs_blk, x_init)
+        return jnp.swapaxes(x_final, 1, 2)
 
     return jax.shard_map(device_fn, mesh=mesh, in_specs=(mat_spec, mat_spec, mat_spec, vec_spec, vec_spec),
                          out_specs=vec_spec, check_vma=False)

time: 161 us -> 138 us (0.86)
  Pallas kernels: 147 us -> 134 us
  local copies, waits for them, and re-layouts: 13.6 us -> 3.97 us
    pallas_call x1, Pallas kernels: 147 us -> 134 us  [device_fn(): pl.pallas_call(functools.partial(kernel, chain_len, rows), out_shape=jax....]
    pallas_call x1 -> x0, local copies, waits for them, and re-layouts: 5.24 us -> none  [device_fn(): pl.pallas_call(functools.partial(kernel, chain_len, rows), out_shape=jax....]
    unnamed x4 -> x1, local copies, waits for them, and re-layouts: 8.39 us -> 3.97 us
where the time goes in v2:
time: 138 us
  Pallas kernels  134 us (97%)
  local copies, waits for them, and re-layouts  3.97 us (3%)
    pallas_call x1, Pallas kernels, device_fn(): pl.pallas_call(functools.partial(kernel, chain_len, rows), out_shape=jax....  134 us
    unnamed x1, local copies, waits for them, and re-layouts  3.97 us

profile of v2, /device:TPU:23, one launch (start us, length us, event | category | flops | bytes accessed | tf_op | source)
XLA Modules:
  0.0 137.9 jit_solution(382850859222377094)
XLA Ops:
  0.0 133.9 %shard_map.55 = f32[8,96,1024]{2,1,0:T(8,128)} custom-call(bf16[8,1024,1024]{2,1,0:T(8,128)(2,1)} %d_hbm.1, bf16[8,1024,1024]{2,1,0:T(8,128)(2,1)} %l_hbm.1, bf16[8,1024,1024]{2,1,0:T(8,128)(2,1)} %u_hbm.1, f32[8,96,1024]{2,1,0:T(8,128)} %bitcast.4, f32[8,96,1024]{2,1,0:T(8,128)} %bitcast.5), custom_call_target="tpu_custom_call" | custom-call | tf_op jit(solution)/shard_map/pallas_call | solution.py:214
  133.9 4.0 %copy.7 = f32[8,1024,96]{1,2,0:T(8,128)} copy(f32[8,1024,96]{1,2,0:T(8,128)} %bitcast.3) | data formatting | bytes 6291456

commit v3 on v2

v3 whole, which is shorter than its diff:
```python
import functools

import jax
import jax.numpy as jnp
from jax import lax
from jax.experimental import pallas as pl
from jax.experimental.pallas import tpu as pltpu
from jax.sharding import PartitionSpec as P

SWEEPS = 4
TILE = 256
MESH = pl.DeviceIdType.MESH
F32, BF16 = jnp.float32, jnp.bfloat16


def dot(x, mat):
    return jnp.dot(x, mat, preferred_element_type=F32)


def kernel(chain_len, rows, d_hbm, l_hbm, u_hbm, f_hbm, x_hbm, out_hbm,
           d_v, l_v, u_v, f_v, g_v, xs, x_raw,
           d_sem, l_sem, u_sem, f_sem, x_sem, out_sem,
           fs_sem, fr_sem, bs_sem, br_sem):
    p = lax.axis_index("row")
    size = d_v.shape[1]
    tiles = size // TILE
    half = size // 2
    halves = (pl.ds(0, half), pl.ds(half, half))
    has_left, has_right = p > 0, p < chain_len - 1
    from_left, from_right = rows, rows + SWEEPS
    last = rows - 1

    def span(t):
        return pl.ds(t * TILE, TILE)

    def mat_copies(i):
        return (pltpu.make_async_copy(l_hbm.at[i], l_v.at[i], l_sem.at[i]),
                pltpu.make_async_copy(d_hbm.at[i], d_v.at[i], d_sem.at[i]),
                pltpu.make_async_copy(u_hbm.at[i], u_v.at[i], u_sem.at[i]))

    def f_copy(i):
        return pltpu.make_async_copy(f_hbm.at[i], f_v.at[i], f_sem.at[i])

    def x_copy(i, slot):
        return pltpu.make_async_copy(x_hbm.at[i], x_raw.at[slot], x_sem.at[slot])

    def out_copy(i):
        return pltpu.make_async_copy(g_v.at[i], out_hbm.at[i], out_sem.at[i])

    def send_right(k, device):
        return pltpu.make_async_remote_copy(
            src_ref=xs.at[last], dst_ref=xs.at[from_left + k], send_sem=fs_sem.at[k], recv_sem=fr_sem.at[k],
            device_id={"row": device}, device_id_type=MESH)

    def send_left(k, device):
        return pltpu.make_async_remote_copy(
            src_ref=xs.at[0], dst_ref=xs.at[from_right + k], send_sem=bs_sem.at[k], recv_sem=br_sem.at[k],
            device_id={"row": device}, device_id_type=MESH)

    x_copy(0, 0).start()
    x_copy(1, 1).start()
    for i in range(2):
        f_copy(i).start()
        for c in mat_copies(i):
            c.start()

    barrier = pltpu.get_barrier_semaphore()

    @pl.when(has_left)
    def _():
        pl.semaphore_signal(barrier, inc=1, device_id={"row": p - 1}, device_id_type=MESH)

    @pl.when(has_right)
    def _():
        pl.semaphore_signal(barrier, inc=1, device_id={"row": p + 1}, device_id_type=MESH)

    pl.semaphore_wait(barrier, has_left.astype(jnp.int32) + has_right.astype(jnp.int32))

    zero = jnp.zeros(xs.shape[1:], BF16)

    @pl.when(jnp.logical_not(has_left))
    def _():
        for k in range(SWEEPS):
            xs[from_left + k] = zero

    @pl.when(jnp.logical_not(has_right))
    def _():
        for k in range(SWEEPS):
            xs[from_right + k] = zero

    def load_x(i, slot):
        x_copy(i, slot).wait()
        xs[i] = x_raw[slot].astype(BF16)

    def transpose_in_place(ref, i):
        def at(a, b):
            return ref.at[i, span(a), span(b)]
        for a in range(tiles):
            at(a, a)[...] = at(a, a)[...].T
            for b in range(a + 1, tiles):
                upper, lower = at(a, b)[...].T, at(b, a)[...].T
                at(a, b)[...] = lower
                at(b, a)[...] = upper

    def ahead(i):
        x = xs[i + 1]
        for h in halves:
            g_v[i, :, h] = f_v[i, :, h] - dot(x, u_v[i, :, h])

    def less_left(base, i, left):
        return [base[i, :, h] - dot(left, l_v[i, :, h]) for h in halves]

    def solve(i, t):
        x = dot(t[0].astype(BF16), d_v[i, halves[0], :]) + dot(t[1].astype(BF16), d_v[i, halves[1], :])
        low = x.astype(BF16)
        xs[i] = low
        g_v[i] = x
        return low

    load_x(0, 0)
    x_copy(2, 0).start()

    @pl.when(has_left)
    def _():
        send_left(0, p - 1).start()

    def load_row(i, end=False):
        slot = lax.rem(i, 2)
        if not end:
            @pl.when(i + 2 < rows)
            def _():
                f_copy(i + 2).start()
                for c in mat_copies(i + 2):
                    c.start()
            load_x(i + 1, 1 - slot)

            @pl.when(i + 3 < rows)
            def _():
                x_copy(i + 3, 1 - slot).start()
        f_copy(i).wait()
        l_c, d_c, u_c = mat_copies(i)
        l_c.wait()
        transpose_in_place(l_v, i)
        d_c.wait()
        transpose_in_place(d_v, i)
        u_c.wait()
        transpose_in_place(u_v, i)
        if not end:
            ahead(i)

    with jax.named_scope("load"):
        @pl.loop(0, rows - 1)
        def _(i):
            load_row(i)
        load_row(last, end=True)

    @pl.loop(0, SWEEPS)
    def _(k):
        final = k == SWEEPS - 1

        def wait_left():
            @pl.when(jnp.logical_and(has_right, k > 0))
            def _():
                send_right(k - 1, p + 1).wait_send()

            @pl.when(has_left)
            def _():
                send_left(k, p - 1).wait_send()
                with jax.named_scope("wait_left"):
                    send_right(k, p - 1).wait_recv()

        def wait_right():
            @pl.when(has_right)
            def _():
                with jax.named_scope("wait_right"):
                    send_left(k, p + 1).wait_recv()

        wait_left()
        left = solve(0, less_left(g_v, 0, xs[from_left + k]))

        @pl.when(jnp.logical_and(has_left, jnp.logical_not(final)))
        def _():
            send_left(k + 1, p - 1).start()

        with jax.named_scope("rows_mid"):
            for i in range(1, last):
                left = solve(i, less_left(g_v, i, left))
            t = less_left(f_v, last, left)

        @pl.when(final)
        def _():
            for i in range(last):
                out_copy(i).start()
        wait_right()
        x = xs[from_right + k]
        solve(last, [t[n] - dot(x, u_v[last, :, h]) for n, h in enumerate(halves)])

        @pl.when(has_right)
        def _():
            send_right(k, p + 1).start()

        with jax.named_scope("ahead"):
            @pl.when(jnp.logical_not(final))
            def _():
                for i in range(last):
                    ahead(i)

    out_copy(last).start()

    @pl.when(has_right)
    def _():
        send_right(SWEEPS - 1, p + 1).wait_send()
    for i in range(rows):
        out_copy(i).wait()


def solution(mesh):
    chain_len = mesh.shape["row"]
    mat_spec = P(("batch", "row"), None, None)
    vec_spec = P(("batch", "row"), None, "col")

    def device_fn(d_inv, l_blk, u_blk, rhs_blk, x_init):
        rhs_blk, x_init = jnp.swapaxes(rhs_blk, 1, 2), jnp.swapaxes(x_init, 1, 2)
        rows, cols, size = rhs_blk.shape
        any_spec = pl.BlockSpec(memory_space=pl.ANY)
        mat = pltpu.VMEM((rows, size, size), BF16)
        vec = pltpu.VMEM((rows, cols, size), F32)
        dma = pltpu.SemaphoreType.DMA
        x_final = pl.pallas_call(
            functools.partial(kernel, chain_len, rows),
            out_shape=jax.ShapeDtypeStruct(rhs_blk.shape, F32),
            in_specs=[any_spec] * 5,
            out_specs=any_spec,
            scratch_shapes=[
                mat, mat, mat, vec, vec,
                pltpu.VMEM((rows + 2 * SWEEPS, cols, size), BF16),
                pltpu.VMEM((2, cols, size), F32),
                dma((rows,)), dma((rows,)), dma((rows,)), dma((rows,)), dma((2,)), dma((rows,)),
                dma((SWEEPS,)), dma((SWEEPS,)), dma((SWEEPS,)), dma((SWEEPS,)),
            ],
            compiler_params=pltpu.CompilerParams(
                collective_id=0, has_side_effects=True, vmem_limit_bytes=67043328),
        )(d_inv, l_blk, u_blk, rhs_blk, x_init)
        return jnp.swapaxes(x_final, 1, 2)

    return jax.shard_map(device_fn, mesh=mesh, in_specs=(mat_spec, mat_spec, mat_spec, vec_spec, vec_spec),
                         out_specs=vec_spec, check_vma=False)
```

time: 138 us -> 127 us (0.920)
  Pallas kernels: 134 us -> 123 us
    pallas_call x1, Pallas kernels: 134 us -> 123 us  [device_fn(): pl.pallas_call(functools.partial(kernel, chain_len, rows), out_shape=jax....]
where the time goes in v3:
time: 127 us
  Pallas kernels  123 us (97%)
  local copies, waits for them, and re-layouts  3.97 us (3%)
    pallas_call x1, Pallas kernels, device_fn(): pl.pallas_call(functools.partial(kernel, chain_len, rows), out_shape=jax....  123 us
    unnamed x1, local copies, waits for them, and re-layouts  3.97 us

profile of v3, /device:TPU:23, one launch (start us, length us, event | category | flops | bytes accessed | tf_op | source)
XLA Modules:
  0.0 127.1 jit_solution(18339835060001738976)
XLA Ops:
  0.0 123.2 %shard_map.55 = f32[8,96,1024]{2,1,0:T(8,128)} custom-call(bf16[8,1024,1024]{2,1,0:T(8,128)(2,1)} %d_hbm.1, bf16[8,1024,1024]{2,1,0:T(8,128)(2,1)} %l_hbm.1, bf16[8,1024,1024]{2,1,0:T(8,128)(2,1)} %u_hbm.1, f32[8,96,1024]{2,1,0:T(8,128)} %bitcast.4, f32[8,96,1024]{2,1,0:T(8,128)} %bitcast.5), custom_call_target="tpu_custom_call" | custom-call | tf_op jit(solution)/shard_map/pallas_call | solution.py:229
  123.2 4.0 %copy.7 = f32[8,1024,96]{1,2,0:T(8,128)} copy(f32[8,1024,96]{1,2,0:T(8,128)} %bitcast.3) | data formatting | bytes 6291456

commit v4 on v3

--- a/solution.py
+++ b/solution.py
@@ -9,6 +9,7 @@
 
 SWEEPS = 4
 TILE = 256
+DEPTH = 3
 MESH = pl.DeviceIdType.MESH
 F32, BF16 = jnp.float32, jnp.bfloat16
 
@@ -24,8 +25,6 @@
     p = lax.axis_index("row")
     size = d_v.shape[1]
     tiles = size // TILE
-    half = size // 2
-    halves = (pl.ds(0, half), pl.ds(half, half))
     has_left, has_right = p > 0, p < chain_len - 1
     from_left, from_right = rows, rows + SWEEPS
     last = rows - 1
@@ -59,7 +58,7 @@
 
     x_copy(0, 0).start()
     x_copy(1, 1).start()
-    for i in range(2):
+    for i in range(DEPTH):
         f_copy(i).start()
         for c in mat_copies(i):
             c.start()
@@ -103,20 +102,21 @@
                 at(b, a)[...] = upper
 
     def ahead(i):
-        x = xs[i + 1]
-        for h in halves:
-            g_v[i, :, h] = f_v[i, :, h] - dot(x, u_v[i, :, h])
-
-    def less_left(base, i, left):
-        return [base[i, :, h] - dot(left, l_v[i, :, h]) for h in halves]
+        g_v[i] = f_v[i] - dot(xs[i + 1], u_v[i])
 
     def solve(i, t):
-        x = dot(t[0].astype(BF16), d_v[i, halves[0], :]) + dot(t[1].astype(BF16), d_v[i, halves[1], :])
+        x = dot(t.astype(BF16), d_v[i])
         low = x.astype(BF16)
         xs[i] = low
         g_v[i] = x
         return low
 
+    def row(i, left):
+        return solve(i, g_v[i] - dot(left, l_v[i]))
+
+    def last_left(left):
+        g_v[last] = f_v[last] - dot(left, l_v[last])
+
     load_x(0, 0)
     x_copy(2, 0).start()
 
@@ -124,35 +124,60 @@
     def _():
         send_left(0, p - 1).start()
 
-    def load_row(i, end=False):
+    def more_loads(i):
         slot = lax.rem(i, 2)
-        if not end:
-            @pl.when(i + 2 < rows)
-            def _():
-                f_copy(i + 2).start()
-                for c in mat_copies(i + 2):
-                    c.start()
-            load_x(i + 1, 1 - slot)
-
-            @pl.when(i + 3 < rows)
-            def _():
-                x_copy(i + 3, 1 - slot).start()
-        f_copy(i).wait()
-        l_c, d_c, u_c = mat_copies(i)
-        l_c.wait()
-        transpose_in_place(l_v, i)
-        d_c.wait()
-        transpose_in_place(d_v, i)
-        u_c.wait()
-        transpose_in_place(u_v, i)
-        if not end:
-            ahead(i)
+
+        @pl.when(i + DEPTH < rows)
+        def _():
+            f_copy(i + DEPTH).start()
+            for c in mat_copies(i + DEPTH):
+                c.start()
+        load_x(i + 1, 1 - slot)
+
+        @pl.when(i + 3 < rows)
+        def _():
+            x_copy(i + 3, 1 - slot).start()
+
+    mats = (l_v, d_v, u_v)
 
     with jax.named_scope("load"):
-        @pl.loop(0, rows - 1)
-        def _(i):
-            load_row(i)
-        load_row(last, end=True)
+        @pl.when(has_left)
+        def _():
+            def load_row(i):
+                f_copy(i).wait()
+                for c, ref in zip(mat_copies(i), mats):
+                    c.wait()
+                    transpose_in_place(ref, i)
+
+            @pl.loop(0, last)
+            def _(i):
+                more_loads(i)
+                load_row(i)
+                ahead(i)
+            load_row(last)
+
+        @pl.when(jnp.logical_not(has_left))
+        def _():
+            def load_row(i, behind):
+                f_copy(i).wait()
+                for c in mat_copies(i):
+                    c.wait()
+                transpose_in_place(u_v, i)
+                behind()
+                transpose_in_place(l_v, i)
+                transpose_in_place(d_v, i)
+
+            more_loads(0)
+            load_row(0, lambda: None)
+            ahead(0)
+
+            @pl.loop(1, last)
+            def _(i):
+                more_loads(i)
+                load_row(i, lambda: row(i - 1, xs[jnp.where(i == 1, from_left, i - 2)]))
+                ahead(i)
+            load_row(last, lambda: row(last - 1, xs[last - 2]))
+            last_left(xs[last - 1])
 
     @pl.loop(0, SWEEPS)
     def _(k):
@@ -175,25 +200,26 @@
                 with jax.named_scope("wait_right"):
                     send_left(k, p + 1).wait_recv()
 
-        wait_left()
-        left = solve(0, less_left(g_v, 0, xs[from_left + k]))
-
-        @pl.when(jnp.logical_and(has_left, jnp.logical_not(final)))
-        def _():
-            send_left(k + 1, p - 1).start()
-
-        with jax.named_scope("rows_mid"):
-            for i in range(1, last):
-                left = solve(i, less_left(g_v, i, left))
-            t = less_left(f_v, last, left)
+        @pl.when(jnp.logical_or(has_left, k > 0))
+        def _():
+            wait_left()
+            left = row(0, xs[from_left + k])
+
+            @pl.when(jnp.logical_and(has_left, jnp.logical_not(final)))
+            def _():
+                send_left(k + 1, p - 1).start()
+
+            with jax.named_scope("rows_mid"):
+                for i in range(1, last):
+                    left = row(i, left)
+                last_left(left)
 
         @pl.when(final)
         def _():
             for i in range(last):
                 out_copy(i).start()
         wait_right()
-        x = xs[from_right + k]
-        solve(last, [t[n] - dot(x, u_v[last, :, h]) for n, h in enumerate(halves)])
+        solve(last, g_v[last] - dot(xs[from_right + k], u_v[last]))
 
         @pl.when(has_right)
         def _():

time: 127 us -> 118 us (0.929)
  Pallas kernels: 123 us -> 114 us
    pallas_call x1, Pallas kernels: 123 us -> 114 us  [device_fn(): pl.pallas_call(functools.partial(kernel, chain_len, rows), out_shape=jax....]
where the time goes in v4:
time: 118 us
  Pallas kernels  114 us (97%)
  local copies, waits for them, and re-layouts  3.97 us (3%)
    pallas_call x1, Pallas kernels, device_fn(): pl.pallas_call(functools.partial(kernel, chain_len, rows), out_shape=jax....  114 us
    unnamed x1, local copies, waits for them, and re-layouts  3.97 us

profile of v4, /device:TPU:23, one launch (start us, length us, event | category | flops | bytes accessed | tf_op | source)
XLA Modules:
  0.0 118.2 jit_solution(14051878775062011604)
XLA Ops:
  0.0 114.2 %shard_map.55 = f32[8,96,1024]{2,1,0:T(8,128)} custom-call(bf16[8,1024,1024]{2,1,0:T(8,128)(2,1)} %d_hbm.1, bf16[8,1024,1024]{2,1,0:T(8,128)(2,1)} %l_hbm.1, bf16[8,1024,1024]{2,1,0:T(8,128)(2,1)} %u_hbm.1, f32[8,96,1024]{2,1,0:T(8,128)} %bitcast.4, f32[8,96,1024]{2,1,0:T(8,128)} %bitcast.5), custom_call_target="tpu_custom_call" | custom-call | tf_op jit(solution)/shard_map/pallas_call | solution.py:255
  114.2 4.0 %copy.7 = f32[8,1024,96]{1,2,0:T(8,128)} copy(f32[8,1024,96]{1,2,0:T(8,128)} %bitcast.3) | data formatting | bytes 6291456

commit v5 on v3

--- a/solution.py
+++ b/solution.py
@@ -24,8 +24,6 @@
     p = lax.axis_index("row")
     size = d_v.shape[1]
     tiles = size // TILE
-    half = size // 2
-    halves = (pl.ds(0, half), pl.ds(half, half))
     has_left, has_right = p > 0, p < chain_len - 1
     from_left, from_right = rows, rows + SWEEPS
     last = rows - 1
@@ -57,13 +55,21 @@
             src_ref=xs.at[0], dst_ref=xs.at[from_right + k], send_sem=bs_sem.at[k], recv_sem=br_sem.at[k],
             device_id={"row": device}, device_id_type=MESH)
 
-    x_copy(0, 0).start()
-    x_copy(1, 1).start()
-    for i in range(2):
+    def load_x(i, slot):
+        x_copy(i, slot).wait()
+        xs[i] = x_raw[slot].astype(BF16)
+
+    def start_row(i):
         f_copy(i).start()
         for c in mat_copies(i):
             c.start()
 
+    @pl.when(has_left)
+    def _():
+        x_copy(0, 0).start()
+    x_copy(1, 1).start()
+    start_row(0)
+
     barrier = pltpu.get_barrier_semaphore()
 
     @pl.when(has_left)
@@ -75,6 +81,13 @@
         pl.semaphore_signal(barrier, inc=1, device_id={"row": p + 1}, device_id_type=MESH)
 
     pl.semaphore_wait(barrier, has_left.astype(jnp.int32) + has_right.astype(jnp.int32))
+
+    @pl.when(has_left)
+    def _():
+        load_x(0, 0)
+        send_left(0, p - 1).start()
+    start_row(1)
+    x_copy(2, 0).start()
 
     zero = jnp.zeros(xs.shape[1:], BF16)
 
@@ -87,10 +100,6 @@
     def _():
         for k in range(SWEEPS):
             xs[from_right + k] = zero
-
-    def load_x(i, slot):
-        x_copy(i, slot).wait()
-        xs[i] = x_raw[slot].astype(BF16)
 
     def transpose_in_place(ref, i):
         def at(a, b):
@@ -103,56 +112,74 @@
                 at(b, a)[...] = upper
 
     def ahead(i):
-        x = xs[i + 1]
-        for h in halves:
-            g_v[i, :, h] = f_v[i, :, h] - dot(x, u_v[i, :, h])
-
-    def less_left(base, i, left):
-        return [base[i, :, h] - dot(left, l_v[i, :, h]) for h in halves]
+        g_v[i] = f_v[i] - dot(xs[i + 1], u_v[i])
 
     def solve(i, t):
-        x = dot(t[0].astype(BF16), d_v[i, halves[0], :]) + dot(t[1].astype(BF16), d_v[i, halves[1], :])
+        x = dot(t.astype(BF16), d_v[i])
         low = x.astype(BF16)
         xs[i] = low
         g_v[i] = x
         return low
 
-    load_x(0, 0)
-    x_copy(2, 0).start()
-
-    @pl.when(has_left)
-    def _():
-        send_left(0, p - 1).start()
-
-    def load_row(i, end=False):
+    def row(i, left):
+        return solve(i, g_v[i] - dot(left, l_v[i]))
+
+    def load_row(i, behind=lambda: None, end=False, skip_l=False):
         slot = lax.rem(i, 2)
+        f_copy(i).wait()
+        for c in mat_copies(i):
+            c.wait()
         if not end:
+            load_x(i + 1, 1 - slot)
+
             @pl.when(i + 2 < rows)
             def _():
-                f_copy(i + 2).start()
-                for c in mat_copies(i + 2):
-                    c.start()
-            load_x(i + 1, 1 - slot)
+                start_row(i + 2)
 
             @pl.when(i + 3 < rows)
             def _():
                 x_copy(i + 3, 1 - slot).start()
-        f_copy(i).wait()
-        l_c, d_c, u_c = mat_copies(i)
-        l_c.wait()
-        transpose_in_place(l_v, i)
-        d_c.wait()
-        transpose_in_place(d_v, i)
-        u_c.wait()
         transpose_in_place(u_v, i)
+        behind()
         if not end:
             ahead(i)
+        if not skip_l:
+            transpose_in_place(l_v, i)
+        transpose_in_place(d_v, i)
 
     with jax.named_scope("load"):
-        @pl.loop(0, rows - 1)
-        def _(i):
-            load_row(i)
-        load_row(last, end=True)
+        @pl.when(has_left)
+        def _():
+            @pl.loop(0, last)
+            def _(i):
+                load_row(i)
+            load_row(last, end=True)
+
+        @pl.when(jnp.logical_not(has_left))
+        def _():
+            load_row(0, skip_l=True)
+            load_row(1, lambda: solve(0, g_v[0]))
+
+            @pl.loop(2, last)
+            def _(i):
+                load_row(i, lambda: row(i - 1, xs[i - 2]))
+            load_row(last, lambda: row(last - 1, xs[last - 2]), end=True)
+
+    def last_right(k):
+        @pl.when(has_right)
+        def _():
+            with jax.named_scope("wait_right"):
+                send_left(k, p + 1).wait_recv()
+        return dot(xs[from_right + k], u_v[last])
+
+    near = jnp.logical_or(lax.rem(p, 2) == 0, jnp.logical_not(has_right))
+
+    with jax.named_scope("last_early"):
+        g_v[last] = f_v[last] - last_right(0)
+
+    @pl.when(jnp.logical_not(has_left))
+    def _():
+        row(last, xs[last - 1])
 
     @pl.loop(0, SWEEPS)
     def _(k):
@@ -169,35 +196,41 @@
                 with jax.named_scope("wait_left"):
                     send_right(k, p - 1).wait_recv()
 
-        def wait_right():
-            @pl.when(has_right)
-            def _():
-                with jax.named_scope("wait_right"):
-                    send_left(k, p + 1).wait_recv()
-
-        wait_left()
-        left = solve(0, less_left(g_v, 0, xs[from_left + k]))
-
-        @pl.when(jnp.logical_and(has_left, jnp.logical_not(final)))
-        def _():
-            send_left(k + 1, p - 1).start()
-
-        with jax.named_scope("rows_mid"):
-            for i in range(1, last):
-                left = solve(i, less_left(g_v, i, left))
-            t = less_left(f_v, last, left)
+        @pl.when(jnp.logical_or(has_left, k > 0))
+        def _():
+            wait_left()
+            left = row(0, xs[from_left + k])
+
+            @pl.when(jnp.logical_and(has_left, jnp.logical_not(final)))
+            def _():
+                send_left(k + 1, p - 1).start()
+
+            early = jnp.logical_or(near, k == 0)
+
+            @pl.when(early)
+            def _():
+                with jax.named_scope("rows_early"):
+                    old = left
+                    for i in range(1, rows):
+                        old = row(i, old)
+
+            @pl.when(jnp.logical_not(early))
+            def _():
+                with jax.named_scope("rows_late"):
+                    old = left
+                    for i in range(1, last):
+                        old = row(i, old)
+                    g_v[last] = f_v[last] - dot(old, l_v[last])
+                solve(last, g_v[last] - last_right(k))
+
+        @pl.when(has_right)
+        def _():
+            send_right(k, p + 1).start()
 
         @pl.when(final)
         def _():
-            for i in range(last):
+            for i in range(rows):
                 out_copy(i).start()
-        wait_right()
-        x = xs[from_right + k]
-        solve(last, [t[n] - dot(x, u_v[last, :, h]) for n, h in enumerate(halves)])
-
-        @pl.when(has_right)
-        def _():
-            send_right(k, p + 1).start()
 
         with jax.named_scope("ahead"):
             @pl.when(jnp.logical_not(final))
@@ -205,7 +238,11 @@
                 for i in range(last):
                     ahead(i)
 
-    out_copy(last).start()
+        @pl.when(jnp.logical_and(near, jnp.logical_not(final)))
+        def _():
+            with jax.named_scope("last_early"):
+                g_v[last] = f_v[last] - last_right(k + 1)
+
 
     @pl.when(has_right)
     def _():

time: 127 us -> 115 us (0.906)
  Pallas kernels: 123 us -> 111 us
    pallas_call x1, Pallas kernels: 123 us -> 111 us  [device_fn(): pl.pallas_call(functools.partial(kernel, chain_len, rows), out_shape=jax....]
where the time goes in v5:
time: 115 us
  Pallas kernels  111 us (97%)
  local copies, waits for them, and re-layouts  3.97 us (3%)
    pallas_call x1, Pallas kernels, device_fn(): pl.pallas_call(functools.partial(kernel, chain_len, rows), out_shape=jax....  111 us
    unnamed x1, local copies, waits for them, and re-layouts  3.97 us

profile of v5, /device:TPU:23, one launch (start us, length us, event | category | flops | bytes accessed | tf_op | source)
XLA Modules:
  0.0 115.0 jit_solution(6801468784581126651)
XLA Ops:
  0.0 111.0 %shard_map.55 = f32[8,96,1024]{2,1,0:T(8,128)} custom-call(bf16[8,1024,1024]{2,1,0:T(8,128)(2,1)} %d_hbm.1, bf16[8,1024,1024]{2,1,0:T(8,128)(2,1)} %l_hbm.1, bf16[8,1024,1024]{2,1,0:T(8,128)(2,1)} %u_hbm.1, f32[8,96,1024]{2,1,0:T(8,128)} %bitcast.4, f32[8,96,1024]{2,1,0:T(8,128)} %bitcast.5), custom_call_target="tpu_custom_call" | custom-call | tf_op jit(solution)/shard_map/pallas_call | solution.py:266
  111.0 4.0 %copy.7 = f32[8,1024,96]{1,2,0:T(8,128)} copy(f32[8,1024,96]{1,2,0:T(8,128)} %bitcast.3) | data formatting | bytes 6291456

commit v6 on v5

--- a/solution.py
+++ b/solution.py
@@ -31,10 +31,14 @@
     def span(t):
         return pl.ds(t * TILE, TILE)
 
-    def mat_copies(i):
-        return (pltpu.make_async_copy(l_hbm.at[i], l_v.at[i], l_sem.at[i]),
-                pltpu.make_async_copy(d_hbm.at[i], d_v.at[i], d_sem.at[i]),
-                pltpu.make_async_copy(u_hbm.at[i], u_v.at[i], u_sem.at[i]))
+    def l_copy(i):
+        return pltpu.make_async_copy(l_hbm.at[i], l_v.at[i], l_sem.at[i])
+
+    def d_copy(i):
+        return pltpu.make_async_copy(d_hbm.at[i], d_v.at[i], d_sem.at[i])
+
+    def u_copy(i):
+        return pltpu.make_async_copy(u_hbm.at[i], u_v.at[i], u_sem.at[i])
 
     def f_copy(i):
         return pltpu.make_async_copy(f_hbm.at[i], f_v.at[i], f_sem.at[i])
@@ -61,14 +65,20 @@
 
     def start_row(i):
         f_copy(i).start()
-        for c in mat_copies(i):
+        for c in (u_copy(i), l_copy(i), d_copy(i)):
             c.start()
 
     @pl.when(has_left)
     def _():
         x_copy(0, 0).start()
     x_copy(1, 1).start()
-    start_row(0)
+    f_copy(0).start()
+    u_copy(0).start()
+    d_copy(0).start()
+
+    @pl.when(has_left)
+    def _():
+        l_copy(0).start()
 
     barrier = pltpu.get_barrier_semaphore()
 
@@ -86,7 +96,10 @@
     def _():
         load_x(0, 0)
         send_left(0, p - 1).start()
-    start_row(1)
+        d_copy(1).start()
+    f_copy(1).start()
+    u_copy(1).start()
+    l_copy(1).start()
     x_copy(2, 0).start()
 
     zero = jnp.zeros(xs.shape[1:], BF16)
@@ -124,10 +137,16 @@
     def row(i, left):
         return solve(i, g_v[i] - dot(left, l_v[i]))
 
-    def load_row(i, behind=lambda: None, end=False, skip_l=False):
+    def last_right(k):
+        @pl.when(has_right)
+        def _():
+            with jax.named_scope("wait_right"):
+                send_left(k, p + 1).wait_recv()
+        return dot(xs[from_right + k], u_v[last])
+
+    def load_row(i, end=False):
         slot = lax.rem(i, 2)
-        f_copy(i).wait()
-        for c in mat_copies(i):
+        for c in (f_copy(i), u_copy(i), l_copy(i), d_copy(i)):
             c.wait()
         if not end:
             load_x(i + 1, 1 - slot)
@@ -140,12 +159,18 @@
             def _():
                 x_copy(i + 3, 1 - slot).start()
         transpose_in_place(u_v, i)
-        behind()
         if not end:
             ahead(i)
-        if not skip_l:
-            transpose_in_place(l_v, i)
+        transpose_in_place(l_v, i)
         transpose_in_place(d_v, i)
+
+    def load_block(copies, ref, i, starts=(), behind=lambda: None):
+        for c in copies:
+            c.wait()
+        for c in starts:
+            c.start()
+        transpose_in_place(ref, i)
+        behind()
 
     with jax.named_scope("load"):
         @pl.when(has_left)
@@ -157,29 +182,58 @@
 
         @pl.when(jnp.logical_not(has_left))
         def _():
-            load_row(0, skip_l=True)
-            load_row(1, lambda: solve(0, g_v[0]))
-
-            @pl.loop(2, last)
+            def before(i):
+                @pl.when(i == 1)
+                def _():
+                    load_block((f_copy(i), u_copy(i)), u_v, i, behind=lambda: solve(0, g_v[0]))
+
+                @pl.when(i > 1)
+                def _():
+                    load_block((f_copy(i), u_copy(i)), u_v, i, behind=lambda: row(i - 1, xs[i - 2]))
+
+            load_x(1, 1)
+            load_block((f_copy(0), u_copy(0)), u_v, 0, (d_copy(1), f_copy(2), x_copy(3, 1)), lambda: ahead(0))
+            load_block((d_copy(0),), d_v, 0, (u_copy(2),))
+
+            @pl.loop(1, last)
             def _(i):
-                load_row(i, lambda: row(i - 1, xs[i - 2]))
-            load_row(last, lambda: row(last - 1, xs[last - 2]), end=True)
-
-    def last_right(k):
-        @pl.when(has_right)
-        def _():
-            with jax.named_scope("wait_right"):
-                send_left(k, p + 1).wait_recv()
-        return dot(xs[from_right + k], u_v[last])
+                slot = lax.rem(i, 2)
+                load_x(i + 1, 1 - slot)
+                l_copy(i + 1).start()
+
+                @pl.when(i + 2 < rows)
+                def _():
+                    f_copy(i + 2).start()
+
+                @pl.when(i + 3 < rows)
+                def _():
+                    x_copy(i + 3, 1 - slot).start()
+                before(i)
+                load_block((l_copy(i),), l_v, i, (d_copy(i + 1),), lambda: ahead(i))
+
+                @pl.when(i + 2 < rows)
+                def _():
+                    u_copy(i + 2).start()
+                load_block((d_copy(i),), d_v, i)
+            l_copy(0).start()
+            load_block((f_copy(last), u_copy(last)), u_v, last, behind=lambda: row(last - 1, xs[last - 2]))
+
+            def last_ahead():
+                g_v[last] = f_v[last] - dot(xs[from_right], u_v[last])
+
+            def last_left():
+                g_v[last] = g_v[last] - dot(xs[last - 1], l_v[last])
+            send_left(0, p + 1).wait_recv()
+            load_block((l_copy(last),), l_v, last, behind=last_ahead)
+            load_block((d_copy(last),), d_v, last, behind=last_left)
+            solve(last, g_v[last])
 
     near = jnp.logical_or(lax.rem(p, 2) == 0, jnp.logical_not(has_right))
 
-    with jax.named_scope("last_early"):
-        g_v[last] = f_v[last] - last_right(0)
-
-    @pl.when(jnp.logical_not(has_left))
-    def _():
-        row(last, xs[last - 1])
+    @pl.when(has_left)
+    def _():
+        with jax.named_scope("last_early"):
+            g_v[last] = f_v[last] - last_right(0)
 
     @pl.loop(0, SWEEPS)
     def _(k):
@@ -207,7 +261,17 @@
 
             early = jnp.logical_or(near, k == 0)
 
-            @pl.when(early)
+            @pl.when(jnp.logical_and(near, final))
+            def _():
+                with jax.named_scope("rows_final"):
+                    old = left
+                    for i in range(1, rows):
+                        old = row(i, old)
+                        if i in (rows // 2, last - 1):
+                            for j in range(0 if i == rows // 2 else rows // 2 + 1, i + 1):
+                                out_copy(j).start()
+
+            @pl.when(jnp.logical_and(early, jnp.logical_not(final)))
             def _():
                 with jax.named_scope("rows_early"):
                     old = left
@@ -227,10 +291,18 @@
         def _():
             send_right(k, p + 1).start()
 
+        @pl.when(jnp.logical_not(jnp.logical_or(near, jnp.logical_not(final))))
+        def _():
+            for i in range(last):
+                out_copy(i).start()
+
         @pl.when(final)
         def _():
-            for i in range(rows):
-                out_copy(i).start()
+            out_copy(last).start()
+
+        @pl.when(jnp.logical_not(jnp.logical_or(has_left, k > 0)))
+        def _():
+            l_copy(0).wait()
 
         with jax.named_scope("ahead"):
             @pl.when(jnp.logical_not(final))

time: 115 us -> 113 us (0.983)
  Pallas kernels: 111 us -> 109 us
    pallas_call x1, Pallas kernels: 111 us -> 109 us  [device_fn(): pl.pallas_call(functools.partial(kernel, chain_len, rows), out_shape=jax....]
where the time goes in v6:
time: 113 us
  Pallas kernels  109 us (96%)
  local copies, waits for them, and re-layouts  3.97 us (4%)
    pallas_call x1, Pallas kernels, device_fn(): pl.pallas_call(functools.partial(kernel, chain_len, rows), out_shape=jax....  109 us
    unnamed x1, local copies, waits for them, and re-layouts  3.97 us

profile of v6, /device:TPU:23, one launch (start us, length us, event | category | flops | bytes accessed | tf_op | source)
XLA Modules:
  0.0 113.0 jit_solution(18368623451175521154)
XLA Ops:
  0.0 109.1 %shard_map.55 = f32[8,96,1024]{2,1,0:T(8,128)} custom-call(bf16[8,1024,1024]{2,1,0:T(8,128)(2,1)} %d_hbm.1, bf16[8,1024,1024]{2,1,0:T(8,128)(2,1)} %l_hbm.1, bf16[8,1024,1024]{2,1,0:T(8,128)(2,1)} %u_hbm.1, f32[8,96,1024]{2,1,0:T(8,128)} %bitcast.4, f32[8,96,1024]{2,1,0:T(8,128)} %bitcast.5), custom_call_target="tpu_custom_call" | custom-call | tf_op jit(solution)/shard_map/pallas_call | solution.py:338
  109.1 4.0 %copy.7 = f32[8,1024,96]{1,2,0:T(8,128)} copy(f32[8,1024,96]{1,2,0:T(8,128)} %bitcast.3) | data formatting | bytes 6291456

commit v7 on v6

--- a/solution.py
+++ b/solution.py
@@ -9,6 +9,7 @@
 
 SWEEPS = 4
 TILE = 256
+CHUNKS = 4
 MESH = pl.DeviceIdType.MESH
 F32, BF16 = jnp.float32, jnp.bfloat16
 
@@ -49,15 +50,32 @@
     def out_copy(i):
         return pltpu.make_async_copy(g_v.at[i], out_hbm.at[i], out_sem.at[i])
 
+    def chunk(c):
+        return pl.ds(c * (size // CHUNKS), size // CHUNKS)
+
     def send_right(k, device):
-        return pltpu.make_async_remote_copy(
-            src_ref=xs.at[last], dst_ref=xs.at[from_left + k], send_sem=fs_sem.at[k], recv_sem=fr_sem.at[k],
-            device_id={"row": device}, device_id_type=MESH)
+        return [pltpu.make_async_remote_copy(
+            src_ref=xs.at[last, :, chunk(c)], dst_ref=xs.at[from_left + k, :, chunk(c)],
+            send_sem=fs_sem.at[k, c], recv_sem=fr_sem.at[k, c],
+            device_id={"row": device}, device_id_type=MESH) for c in range(CHUNKS)]
 
     def send_left(k, device):
-        return pltpu.make_async_remote_copy(
-            src_ref=xs.at[0], dst_ref=xs.at[from_right + k], send_sem=bs_sem.at[k], recv_sem=br_sem.at[k],
-            device_id={"row": device}, device_id_type=MESH)
+        return [pltpu.make_async_remote_copy(
+            src_ref=xs.at[0, :, chunk(c)], dst_ref=xs.at[from_right + k, :, chunk(c)],
+            send_sem=bs_sem.at[k, c], recv_sem=br_sem.at[k, c],
+            device_id={"row": device}, device_id_type=MESH) for c in range(CHUNKS)]
+
+    def start(copies):
+        for c in copies:
+            c.start()
+
+    def sent(copies):
+        for c in copies:
+            c.wait_send()
+
+    def arrived(copies):
+        for c in copies:
+            c.wait_recv()
 
     def load_x(i, slot):
         x_copy(i, slot).wait()
@@ -95,7 +113,7 @@
     @pl.when(has_left)
     def _():
         load_x(0, 0)
-        send_left(0, p - 1).start()
+        start(send_left(0, p - 1))
         d_copy(1).start()
     f_copy(1).start()
     u_copy(1).start()
@@ -141,7 +159,7 @@
         @pl.when(has_right)
         def _():
             with jax.named_scope("wait_right"):
-                send_left(k, p + 1).wait_recv()
+                arrived(send_left(k, p + 1))
         return dot(xs[from_right + k], u_v[last])
 
     def load_row(i, end=False):
@@ -223,11 +241,12 @@
 
             def last_left():
                 g_v[last] = g_v[last] - dot(xs[last - 1], l_v[last])
-            send_left(0, p + 1).wait_recv()
+            arrived(send_left(0, p + 1))
             load_block((l_copy(last),), l_v, last, behind=last_ahead)
             load_block((d_copy(last),), d_v, last, behind=last_left)
             solve(last, g_v[last])
 
+    far_left = jnp.logical_and(lax.rem(p, 2) == 0, has_left)
     near = jnp.logical_or(lax.rem(p, 2) == 0, jnp.logical_not(has_right))
 
     @pl.when(has_left)
@@ -239,32 +258,46 @@
     def _(k):
         final = k == SWEEPS - 1
 
-        def wait_left():
+        @pl.when(jnp.logical_or(has_left, k > 0))
+        def _():
             @pl.when(jnp.logical_and(has_right, k > 0))
             def _():
-                send_right(k - 1, p + 1).wait_send()
+                sent(send_right(k - 1, p + 1))
 
             @pl.when(has_left)
             def _():
-                send_left(k, p - 1).wait_send()
-                with jax.named_scope("wait_left"):
-                    send_right(k, p - 1).wait_recv()
-
-        @pl.when(jnp.logical_or(has_left, k > 0))
-        def _():
-            wait_left()
-            left = row(0, xs[from_left + k])
+                sent(send_left(k, p - 1))
+
+            @pl.when(far_left)
+            def _():
+                with jax.named_scope("first_far"):
+                    t = g_v[0]
+                    for c, copy in enumerate(send_right(k, p - 1)):
+                        copy.wait_recv()
+                        t = t - dot(xs[from_left + k, :, chunk(c)], l_v[0, chunk(c), :])
+                        if c < CHUNKS - 1:
+                            g_v[0] = t
+                            t = g_v[0]
+                    solve(0, t)
+
+            @pl.when(jnp.logical_not(far_left))
+            def _():
+                @pl.when(has_left)
+                def _():
+                    with jax.named_scope("wait_left"):
+                        arrived(send_right(k, p - 1))
+                row(0, xs[from_left + k])
 
             @pl.when(jnp.logical_and(has_left, jnp.logical_not(final)))
             def _():
-                send_left(k + 1, p - 1).start()
+                start(send_left(k + 1, p - 1))
 
             early = jnp.logical_or(near, k == 0)
 
             @pl.when(jnp.logical_and(near, final))
             def _():
                 with jax.named_scope("rows_final"):
-                    old = left
+                    old = xs[0]
                     for i in range(1, rows):
                         old = row(i, old)
                         if i in (rows // 2, last - 1):
@@ -274,14 +307,14 @@
             @pl.when(jnp.logical_and(early, jnp.logical_not(final)))
             def _():
                 with jax.named_scope("rows_early"):
-                    old = left
+                    old = xs[0]
                     for i in range(1, rows):
                         old = row(i, old)
 
             @pl.when(jnp.logical_not(early))
             def _():
                 with jax.named_scope("rows_late"):
-                    old = left
+                    old = xs[0]
                     for i in range(1, last):
                         old = row(i, old)
                     g_v[last] = f_v[last] - dot(old, l_v[last])
@@ -289,7 +322,7 @@
 
         @pl.when(has_right)
         def _():
-            send_right(k, p + 1).start()
+            start(send_right(k, p + 1))
 
         @pl.when(jnp.logical_not(jnp.logical_or(near, jnp.logical_not(final))))
         def _():
@@ -318,9 +351,22 @@
 
     @pl.when(has_right)
     def _():
-        send_right(SWEEPS - 1, p + 1).wait_send()
+        sent(send_right(SWEEPS - 1, p + 1))
     for i in range(rows):
         out_copy(i).wait()
+
+
+def write_out(src, out, buf, in_sem, out_sem):
+    n = src.shape[0]
+    ins = [pltpu.make_async_copy(src.at[i], buf.at[i], in_sem.at[i]) for i in range(n)]
+    outs = [pltpu.make_async_copy(buf.at[i], out.at[i], out_sem.at[i]) for i in range(n)]
+    for c in ins:
+        c.start()
+    for i in range(n):
+        ins[i].wait()
+        outs[i].start()
+    for c in outs:
+        c.wait()
 
 
 def solution(mesh):
@@ -345,11 +391,18 @@
                 pltpu.VMEM((rows + 2 * SWEEPS, cols, size), BF16),
                 pltpu.VMEM((2, cols, size), F32),
                 dma((rows,)), dma((rows,)), dma((rows,)), dma((rows,)), dma((2,)), dma((rows,)),
-                dma((SWEEPS,)), dma((SWEEPS,)), dma((SWEEPS,)), dma((SWEEPS,)),
+                *[dma((SWEEPS, CHUNKS))] * 4,
             ],
             compiler_params=pltpu.CompilerParams(
                 collective_id=0, has_side_effects=True, vmem_limit_bytes=67043328),
         )(d_inv, l_blk, u_blk, rhs_blk, x_init)
+        x_final = pl.pallas_call(
+            write_out,
+            out_shape=jax.ShapeDtypeStruct(rhs_blk.shape, F32),
+            in_specs=[any_spec],
+            out_specs=any_spec,
+            scratch_shapes=[vec, dma((rows,)), dma((rows,))],
+        )(x_final)
         return jnp.swapaxes(x_final, 1, 2)
 
     return jax.shard_map(device_fn, mesh=mesh, in_specs=(mat_spec, mat_spec, mat_spec, vec_spec, vec_spec),

time: 113 us -> 112 us (level)
  local copies, waits for them, and re-layouts: 3.97 us -> 0 us
  Pallas kernels: 109 us -> 111 us
    unnamed x1 -> x0, local copies, waits for them, and re-layouts: 3.97 us -> none
    pallas_call x0 -> x1, Pallas kernels: none -> 2.79 us  [device_fn(): pl.pallas_call(write_out, out_shape=jax.ShapeDtypeStruct(rhs_blk.shape, F...]
where the time goes in v7:
time: 112 us
  Pallas kernels  111 us (99%)
    pallas_call x1, Pallas kernels, device_fn(): pl.pallas_call(functools.partial(kernel, chain_len, rows), out_shape=jax....  109 us
    pallas_call x1, Pallas kernels, device_fn(): pl.pallas_call(write_out, out_shape=jax.ShapeDtypeStruct(rhs_blk.shape, F...  2.79 us

profile of v7, /device:TPU:23, one launch (start us, length us, event | category | flops | bytes accessed | tf_op | source)
XLA Modules:
  0.0 111.6 jit_solution(7643483416143464180)
XLA Ops:
  0.0 108.6 %shard_map.55.src = f32[8,96,1024]{2,1,0:T(8,128)} custom-call(bf16[8,1024,1024]{2,1,0:T(8,128)(2,1)} %d_hbm.1, bf16[8,1024,1024]{2,1,0:T(8,128)(2,1)} %l_hbm.1, bf16[8,1024,1024]{2,1,0:T(8,128)(2,1)} %u_hbm.1, f32[8,96,1024]{2,1,0:T(8,128)} %bitcast.3, f32[8,96,1024]{2,1,0:T(8,128)} %bitcast.4), custom_call_target="tpu_custom_call" | custom-call | tf_op jit(solution)/shard_map/pallas_call | solution.py:384
  108.6 2.8 %shard_map.56 = f32[8,96,1024]{2,1,0:T(8,128)} custom-call(f32[8,96,1024]{2,1,0:T(8,128)} %shard_map.55.src), custom_call_target="tpu_custom_call" | custom-call | tf_op jit(solution)/shard_map/pallas_call | solution.py:399
